TPU v7x, 32 devices: a whole 2x2x4 slice. The times are simulated.
32 devices in a mesh: dp: 4 (over x, y), sp: 8 (over z, core).
Axes of the slice: x: 2, y: 2, z: 4, core: 2. Of those that a mesh axis runs over, the one named last changes fastest.
Arguments:
- q: bfloat16 [128, 16, 128], P('dp'), parts along dimension 0
- k: bfloat16 [128, 4096, 16, 128], P('dp', 'sp'), parts along dimension 0
- v: bfloat16 [128, 4096, 16, 128], P('dp', 'sp'), parts along dimension 0
Outputs:
- q: bfloat16 [128, 16, 128], P('dp'), parts along dimension 0
There are 4 independent parts. A program takes and returns all parts, laid end to end along the dimension named above; each array names one.
All inputs are finite; a program needn't handle non-finite values.
Results may differ from a plain program's by a relative error of at most 0.012.
Values are sent between devices in bfloat16 or wider.
A program may use at most 2 GiB of HBM per device.

v0:
```python
import jax
import jax.numpy as jnp
from jax import lax
from jax.sharding import PartitionSpec as P


def einsum(form, a, b):
    return jnp.einsum(form, a.astype(jnp.float32), b.astype(jnp.float32))


def part_of(q, k, v):
    grouped = q.reshape(q.shape[0], k.shape[2], -1, q.shape[2])
    scores = einsum("bgsd,bugd->bgsu", grouped, k) * q.shape[2] ** -0.5
    high = jnp.max(scores, -1, keepdims=True)
    weights = jnp.exp(scores - high)
    seen = einsum("bgsu,bugd->bgsd", weights.astype(jnp.bfloat16), v)
    return jnp.concatenate([seen, jnp.sum(weights, -1, keepdims=True), high], -1)


def together(parts):
    seen, total, high = parts[..., :-2], parts[..., -2:-1], parts[..., -1:]
    scale = jnp.exp(high - jnp.max(high, 0))
    return (jnp.sum(seen * scale, 0) / jnp.sum(total * scale, 0)).astype(jnp.bfloat16)


def solution(mesh):
    def step(q, k, v):
        return together(lax.all_gather(part_of(q, k, v), "sp")).reshape(q.shape)

    return jax.shard_map(
        step,
        mesh=mesh,
        in_specs=(P("dp", None, None), P("dp", "sp", None, None), P("dp", "sp", None, None)),
        out_specs=P("dp", None, None),
        check_vma=False,
    )
```

profile of v0, /device:TPU:0, one launch (start us, length us, event | category | flops | bytes accessed | tf_op | source)
XLA Modules:
  0.0 139.0 jit_solution(13881640539431039640)
XLA Ops:
  6.5 0.0 all-gather.3.cloned.1.call-start
  6.5 31.9 %fusion.2 = f32[32,16,1,512]{3,2,1,0:T(1,128)S(1)} fusion(bf16[32,512,16,128]{3,2,1,0:T(8,128)(2,1)} %param.4, bf16[32,16,128,1]{2,1,0,3:T(8,128)(2,1)} %bitcast.24), kind=kOutput, calls=%fused_computation.2 | convolution fusion | flops 67108864 | bytes 68288512 | tf_op jit(solution)/shard_map/bgsd,bugd->bgsu/dot_general | solution.py:8
  38.5 0.2 fusion.9
  38.6 0.3 fusion.10
  39.0 0.3 copy.23
  39.2 0.3 copy.22
  39.5 32.6 %fusion = f32[32,16,1,128]{3,2,1,0:T(1,128)S(1)} fusion(bf16[32,512,16,128]{3,2,1,0:T(8,128)(2,1)} %param.5, bf16[32,16,512,1]{2,1,0,3:T(8,128)(2,1)S(1)} %get-tuple-element.7), kind=kOutput, calls=%fused_computation | convolution fusion | flops 67108864 | bytes 67895296 | tf_op jit(solution)/shard_map/bgsu,bugd->bgsd/dot_general | solution.py:8
  72.1 0.9 pad_maximum_fusion
  73.0 0.0 all-gather.3.cloned.1.call-update
  73.1 49.4 %all-gather.3.cloned.1.call-done = f32[256,16,1,130]{3,1,2,0:T(8,128)} async-done(((f32[32,16,1,130]{3,1,2,0:T(8,128)}), f32[256,16,1,130]{3,1,2,0:T(8,128)}) %all-gather.3.cloned.1.call-update) | async-done | bytes 2129936 | tf_op jit(solution)/shard_map/all_gather | solution.py:28
  122.5 2.3 %slice_reduce_fusion = f32[32,16]{1,0:T(8,128)S(1)} fusion(f32[8,32,16,1,130]{4,2,1,0,3:T(8,128)} %bitcast.21), kind=kLoop, calls=%fused_computation.9 | loop fusion | flops 3584 | bytes 18432 | tf_op jit(solution)/shard_map/reduce_max | solution.py:22
  124.8 3.0 %fusion.4 = (f32[32,16]{1,0:T(8,128)S(1)}, f32[8,32,16,1,1]{4,2,1,0,3:T(8,128)S(1)}) fusion(f32[8,32,16,1,130]{4,2,1,0,3:T(8,128)} %bitcast.22, f32[32,16]{1,0:T(8,128)S(1)} %slice_reduce_fusion), kind=kLoop, calls=%fused_computation.5 | loop fusion | flops 11776 | bytes 53248 | tf_op jit(solution)/shard_map/reduce_sum | solution.py:23
  127.8 1.6 %copy.36 = f32[8,32,16,1,1]{2,1,0,3,4:T(8,128)S(1)} copy(f32[8,32,16,1,1]{4,2,1,0,3:T(8,128)S(1)} %get-tuple-element.6) | data formatting | bytes 32768 | tf_op jit(solution)/shard_map/mul | solution.py:23
  129.3 2.0 %fusion.5 = f32[32,16,128]{2,1,0:T(8,128)S(1)} fusion(f32[8,32,16,1,130]{4,2,1,0,3:T(8,128)} %bitcast.23, f32[8,32,16]{2,1,0:T(8,128)S(1)} %bitcast.25), kind=kLoop, calls=%fused_computation.7 | loop fusion | flops 983040 | bytes 2375680 | tf_op jit(solution)/shard_map/reduce_sum | solution.py:23
  131.3 0.8 divide_convert_fusion
Async XLA Ops:
  6.5 115.9 %all-gather.3.cloned.1.call-start = ((), (), s32[]{:S(2)}) async-start(), calls=%async_computation | async-start | bytes 4718592 | tf_op jit(solution)/shard_map/all_gather | solution.py:28
Sparse Core Ops, SparseCore 0:
  73.2 49.2 all-gather.2
where the time goes:
time: 139 us
  matrix products  64.5 us (46%)
  waiting for transfers between devices  49.4 us (36%)
  between operations  13.4 us (10%)
  other arithmetic  9.52 us (7%)
  local copies, waits for them, and re-layouts  2.08 us (1%)
    dot_general x2, matrix products, einsum(): return jnp.einsum(form, a.astype(jnp.float32), b.astype(jnp.float32))  64.5 us
    all_gather x1, waiting for transfers between devices, step(): return together(lax.all_gather(part_of(q, k, v), 'sp')).reshape(q.shape)  49.4 us
    reduce_sum x1, other arithmetic, together(): jnp.sum(total * scale, 0)  2.99 us
  transfers between devices with their start and end apart: 1, of which 1 were waited for; matrix products, arithmetic and copies ran while one was open for 0% of the time, Pallas kernels for 0%

commit v1 on v0

v1 whole, which is shorter than its diff:
```python
import functools

import jax
import jax.numpy as jnp
from jax import lax
from jax.experimental import pallas as pl
from jax.experimental.pallas import tpu as pltpu
from jax.sharding import PartitionSpec as P

SLOTS = 6
TILE = 8
PER = 4


def attend(n, q_ref, k_hbm, v_hbm, o_ref, k_buf, v_buf, s_ref, p_ref, part, stat, last_part, last_stat, k_sem, v_sem,
           send_sem, part_sem, stat_sem, last_send_sem, last_part_sem, last_stat_sem):
    batch, tokens, heads, head = k_hbm.shape
    runs = tokens // TILE
    groups = batch // PER - 1
    me = lax.axis_index("sp")
    scale = head**-0.5
    lanes = lax.broadcasted_iota(jnp.int32, (heads, TILE * heads), 1)
    mine = lanes % heads == lax.broadcasted_iota(jnp.int32, (heads, TILE * heads), 0)
    lane = lax.broadcasted_iota(jnp.int32, (8, 128), 1)

    def k_copy(b):
        slot = lax.rem(b, SLOTS)
        return pltpu.make_async_copy(k_hbm.at[b], k_buf.at[slot], k_sem.at[slot])

    def v_copy(b):
        slot = lax.rem(b, SLOTS)
        return pltpu.make_async_copy(v_hbm.at[b], v_buf.at[slot], v_sem.at[slot])

    def scores(b):
        keys = k_buf.at[lax.rem(b, SLOTS)].reshape(runs, TILE, heads, head)
        query = q_ref[b]
        none = jnp.zeros_like(query)
        high = jnp.full((heads, TILE * heads), -jnp.inf, jnp.float32)
        step = 16
        for m in range(0, runs, step):
            total = None
            for j in range(0, TILE, 2):
                pair = jnp.concatenate([keys[m : m + step, j + c].reshape(step * heads, head) for c in range(2)], 1)
                spread = jnp.concatenate(
                    [jnp.concatenate([query if r == j + c else none for c in range(2)], 1) for r in range(TILE)], 0
                )
                term = lax.dot_general(pair, spread, (((1,), (1,)), ((), ())), preferred_element_type=jnp.float32)
                total = term if total is None else total + term
            total = jnp.where(mine[None], total.reshape(step, heads, TILE * heads), -jnp.inf)
            s_ref[m : m + step] = total
            high = jnp.maximum(high, jnp.max(total, 0))
        return jnp.max(high, 1, keepdims=True) * scale

    def weights(high):
        total = jnp.zeros((heads, TILE * heads), jnp.float32)
        for m in range(runs):
            weight = jnp.exp(s_ref[m] * scale - high)
            total = total + weight
            p_ref[m] = weight.astype(jnp.bfloat16)
        return jnp.sum(total, 1, keepdims=True)

    def values(b):
        rows = v_buf.at[lax.rem(b, SLOTS)].reshape(tokens * heads, head)
        half, deep = tokens * heads // 2, 2 * TILE * heads
        total = None
        for t in range(runs // 4):
            weight = jnp.concatenate(
                [jnp.concatenate([p_ref[x + 2 * t], p_ref[x + 2 * t + 1]], 1) for x in (0, runs // 2)], 0
            )
            value = jnp.concatenate([rows[x + deep * t : x + deep * (t + 1)] for x in (0, half)], 1)
            term = jnp.dot(weight, value, preferred_element_type=jnp.float32)
            total = term if total is None else total + term
        return total[:heads, :head] + total[heads:, head:]

    def noted(table, i, high, total):
        for part_of_heads in range(2):
            rows = slice(8 * part_of_heads, 8 * part_of_heads + 8)
            table = jnp.where(lane == 2 * i + part_of_heads, high[rows], table)
            table = jnp.where(lane == 64 + 2 * i + part_of_heads, total[rows], table)
        return table

    def sends(parts, stats, g, send, part_recv, stat_recv):
        copies = []
        for r in range(1, n):
            peer = {"sp": lax.rem(me + r, n)}
            for buf, recv, s in ((parts, part_recv, 0), (stats, stat_recv, 1)):
                copies.append(
                    pltpu.make_async_remote_copy(
                        src_ref=buf.at[g, me],
                        dst_ref=buf.at[g, me],
                        send_sem=send.at[s],
                        recv_sem=recv.at[g],
                        device_id=peer,
                        device_id_type=pl.DeviceIdType.MESH,
                    )
                )
        return copies

    def arrived(parts, stats, g, part_recv, stat_recv):
        pltpu.make_async_copy(parts.at[g, : n - 1], parts.at[g, : n - 1], part_recv.at[g]).wait()
        pltpu.make_async_copy(stats.at[g, : n - 1], stats.at[g, : n - 1], stat_recv.at[g]).wait()

    def together(parts, stats, g, first, count):
        tables = [stats[g, d] for d in range(n)]
        high = functools.reduce(jnp.maximum, tables)
        shares = [jnp.exp(t - high) for t in tables]
        total = functools.reduce(jnp.add, [pltpu.roll(t, 64, 1) * s for t, s in zip(tables, shares)])
        for i in range(count):
            out = []
            for x in range(2):
                column = 2 * i + x
                seen = None
                for d in range(n):
                    rows = slice(i * heads + 8 * x, i * heads + 8 * x + 8)
                    term = parts[g, d, i * heads : (i + 1) * heads].astype(jnp.float32)[8 * x : 8 * x + 8] * shares[d][:, column : column + 1]
                    seen = term if seen is None else seen + term
                out.append(seen / total[:, column : column + 1])
            o_ref[first + i] = jnp.concatenate(out, 0).astype(jnp.bfloat16)

    barrier = pltpu.get_barrier_semaphore()
    for r in range(1, n):
        pl.semaphore_signal(barrier, inc=1, device_id={"sp": lax.rem(me + r, n)}, device_id_type=pl.DeviceIdType.MESH)
    for b in range(SLOTS):
        k_copy(b).start()
        if b:
            v_copy(b - 1).start()

    def more(b):
        @pl.when(b + SLOTS < batch)
        def _():
            k_copy(b + SLOTS).start()

        @pl.when(b + SLOTS - 1 < batch)
        def _():
            v_copy(b + SLOTS - 1).start()

    k_copy(0).wait()
    high = scores(0)
    total = weights(high)
    more(0)
    pl.semaphore_wait(barrier, n - 1)

    def sequence(b, high, total):
        k_copy(b + 1).wait()
        v_copy(b).wait()
        next_high = scores(b + 1)
        seen = values(b)
        next_total = weights(next_high)
        more(b + 1)
        return seen, next_high, next_total

    def group(g, carry):
        high, total = carry
        table = jnp.zeros((8, 128), jnp.float32)
        for i in range(PER):
            table = noted(table, i, high, total)
            seen, high, total = sequence(g * PER + i, high, total)
            part[g, me, i * heads : (i + 1) * heads] = seen.astype(jnp.bfloat16)
        stat[g, me] = table
        for copy in sends(part, stat, g, send_sem, part_sem, stat_sem):
            copy.start()

        @pl.when(g > 0)
        def _():
            arrived(part, stat, g - 1, part_sem, stat_sem)
            together(part, stat, g - 1, (g - 1) * PER, PER)

        return high, total

    high, total = lax.fori_loop(0, groups, group, (high, total))
    for i in range(PER):
        b = groups * PER + i
        last_stat[i, me] = noted(jnp.zeros((8, 128), jnp.float32), 0, high, total)
        if i < PER - 1:
            seen, high, total = sequence(b, high, total)
        else:
            v_copy(b).wait()
            seen = values(b)
        last_part[i, me] = seen.astype(jnp.bfloat16)
        for copy in sends(last_part, last_stat, i, last_send_sem, last_part_sem, last_stat_sem):
            copy.start()
    arrived(part, stat, groups - 1, part_sem, stat_sem)
    together(part, stat, groups - 1, (groups - 1) * PER, PER)
    for i in range(PER):
        arrived(last_part, last_stat, i, last_part_sem, last_stat_sem)
        together(last_part, last_stat, i, groups * PER + i, 1)
    for parts, stats, send in ((part, stat, send_sem), (last_part, last_stat, last_send_sem)):
        for s, buf in enumerate((parts, stats)):
            pltpu.make_async_copy(buf.at[:, : n - 1], buf.at[:, : n - 1], send.at[s]).wait()


def solution(mesh):
    n = mesh.shape["sp"]

    def step(q, k, v):
        batch, tokens, heads, head = k.shape
        groups = batch // PER - 1
        anywhere, vmem = pl.BlockSpec(memory_space=pl.ANY), pl.BlockSpec(memory_space=pltpu.VMEM)
        return pl.pallas_call(
            functools.partial(attend, n),
            out_shape=jax.ShapeDtypeStruct(q.shape, q.dtype),
            in_specs=[vmem, anywhere, anywhere],
            out_specs=vmem,
            scratch_shapes=[
                pltpu.VMEM((SLOTS, tokens, heads, head), jnp.bfloat16),
                pltpu.VMEM((SLOTS, tokens, heads, head), jnp.bfloat16),
                pltpu.VMEM((tokens // TILE, heads, TILE * heads), jnp.float32),
                pltpu.VMEM((tokens // TILE, heads, TILE * heads), jnp.bfloat16),
                pltpu.VMEM((groups, n, PER * heads, head), jnp.bfloat16),
                pltpu.VMEM((groups, n, 8, 128), jnp.float32),
                pltpu.VMEM((PER, n, heads, head), jnp.bfloat16),
                pltpu.VMEM((PER, n, 8, 128), jnp.float32),
                pltpu.SemaphoreType.DMA((SLOTS,)),
                pltpu.SemaphoreType.DMA((SLOTS,)),
                pltpu.SemaphoreType.DMA((2,)),
                pltpu.SemaphoreType.DMA((groups,)),
                pltpu.SemaphoreType.DMA((groups,)),
                pltpu.SemaphoreType.DMA((2,)),
                pltpu.SemaphoreType.DMA((PER,)),
                pltpu.SemaphoreType.DMA((PER,)),
            ],
            compiler_params=pltpu.CompilerParams(
                vmem_limit_bytes=60 << 20, collective_id=0, has_side_effects=True
            ),
            name="attend",
        )(q, k, v)

    return jax.shard_map(
        step,
        mesh=mesh,
        in_specs=(P("dp", None, None), P("dp", "sp", None, None), P("dp", "sp", None, None)),
        out_specs=P("dp", None, None),
        check_vma=False,
    )
```

time: 139 us -> 56.3 us (0.41)
  matrix products: 64.5 us -> 0 us
  Pallas kernels: 0 us -> 54.6 us
  waiting for transfers between devices: 49.4 us -> 0 us
  between operations: 13.4 us -> 0.01 us
  other arithmetic: 9.52 us -> 0 us
    dot_general x2 -> x0, matrix products: 64.5 us -> none  [einsum(): return jnp.einsum(form, a.astype(jnp.float32), b.astype(jnp.float32))]
    pallas_call x0 -> x1, Pallas kernels: none -> 54.6 us  [step(): pl.pallas_call(functools.partial(attend, n), out_shape=jax.ShapeDtypeStru...]
    all_gather x1 -> x0, waiting for transfers between devices: 49.4 us -> none  [step(): return together(lax.all_gather(part_of(q, k, v), 'sp')).reshape(q.shape)]
    reduce_sum x2 -> x0, other arithmetic: 5 us -> none  [the longest x1 2.99 us: together(): jnp.sum(total * scale, 0)]
    reduce_max x2 -> x0, other arithmetic: 2.46 us -> none  [the longest x1 2.29 us: together(): scale = jnp.exp(high - jnp.max(high, 0))]
    unnamed x0 -> x1, local copies, waits for them, and re-layouts: none -> 1.57 us
    mul x1 -> x0, local copies, waits for them, and re-layouts: 1.56 us -> none  [together(): seen * scale]
  transfers between devices with their start and end apart: 1 -> 0, of which waited for: 1 -> 0; matrix products, arithmetic and copies ran while one was open for 0% -> 0% of each run, Pallas kernels for 0% -> 0%
where the time goes in v1:
time: 56.3 us; the launch traced here: 56.1 us
  Pallas kernels  54.6 us (97%)
  local copies, waits for them, and re-layouts  1.57 us (3%)
    pallas_call x1, Pallas kernels, step(): pl.pallas_call(functools.partial(attend, n), out_shape=jax.ShapeDtypeStru...  54.6 us
    unnamed x1, local copies, waits for them, and re-layouts  1.57 us

profile of v1, /device:TPU:0, one launch (start us, length us, event | category | flops | bytes accessed | tf_op | source)
XLA Modules:
  0.0 56.1 jit_solution(7349124311912598530)
XLA Ops:
  0.0 54.6 %attend.1 = bf16[32,16,128]{2,1,0:T(8,128)(2,1)} custom-call(bf16[32,16,128]{2,1,0:T(8,128)(2,1)} %q_ref.1, bf16[32,512,16,128]{3,2,1,0:T(8,128)(2,1)} %k_hbm.1, bf16[32,512,16,128]{3,2,1,0:T(8,128)(2,1)} %v_hbm.1), custom_call_target="tpu_custom_call" | custom-call | tf_op jit(solution)/shard_map/attend/pallas_call | solution.py:199
  54.6 1.6 %copy.5 = bf16[32,16,128]{2,1,0:T(8,128)(2,1)} copy(bf16[32,16,128]{2,1,0:T(8,128)(2,1)} %attend.1) | data formatting | bytes 262144

commit v2 on v0

v2 whole, which is shorter than its diff:
```python
import functools
import math

import jax
import jax.numpy as jnp
from jax import lax
from jax.experimental import pallas as pl
from jax.experimental.pallas import tpu as pltpu
from jax.sharding import PartitionSpec as P

TILE = 8
STEP = 32
PAIR = 2
LAG = 6
SLOTS = 8


def attend(n, q_hbm, k_hbm, v_hbm, o_ref, q_ref, k_buf, v_buf, s_buf, p_buf, part, last, stat, q_sem, k_sem, v_sem,
           send_sem, part_sem, last_sem, stat_sem):
    batch, tokens, heads, head = k_hbm.shape
    runs = tokens // TILE
    pairs = batch // PAIR - 1
    half = batch // 2
    me = lax.axis_index("sp")
    scale = head**-0.5 / math.log(2)
    lanes = lax.broadcasted_iota(jnp.int32, (heads, TILE * heads), 1)
    mine = lanes % heads == lax.broadcasted_iota(jnp.int32, (heads, TILE * heads), 0)
    lane = lax.broadcasted_iota(jnp.int32, (8, 128), 1)

    def k_copy(b):
        slot = lax.rem(b, SLOTS)
        return pltpu.make_async_copy(k_hbm.at[b], k_buf.at[slot], k_sem.at[slot])

    def v_copy(b):
        slot = lax.rem(b, SLOTS)
        return pltpu.make_async_copy(v_hbm.at[b], v_buf.at[slot], v_sem.at[slot])

    def scores(b, s_ref):
        keys = k_buf.at[lax.rem(b, SLOTS)].reshape(runs, TILE, heads, head)
        query = q_ref[b]
        none = jnp.zeros_like(query)
        high = jnp.full((heads, TILE * heads), -jnp.inf, jnp.float32)
        for m in range(0, runs, STEP):
            total = None
            for j in range(0, TILE, 2):
                two = jnp.concatenate([keys[m : m + STEP, j + c].reshape(STEP * heads, head) for c in range(2)], 1)
                spread = jnp.concatenate(
                    [jnp.concatenate([query if r == j + c else none for c in range(2)], 1) for r in range(TILE)], 0
                )
                term = lax.dot_general(two, spread, (((1,), (1,)), ((), ())), preferred_element_type=jnp.float32)
                total = term if total is None else total + term
            total = jnp.where(mine[None], total.reshape(STEP, heads, TILE * heads), -jnp.inf)
            s_ref[m : m + STEP] = total
            high = jnp.maximum(high, jnp.max(total, 0))
        return jnp.max(high, 1, keepdims=True) * scale

    def weights(high, s_ref, p_ref):
        total = jnp.zeros((heads, TILE * heads), jnp.float32)
        high = jnp.broadcast_to(high, total.shape)
        for m in range(runs):
            weight = jnp.exp2(s_ref[m] * scale - high)
            total = total + weight
            p_ref[m] = weight.astype(jnp.bfloat16)
        return jnp.sum(total, 1, keepdims=True)

    def values(b, p_ref):
        rows = v_buf.at[lax.rem(b, SLOTS)].reshape(tokens * heads, head)
        deep = 2 * TILE * heads
        total = None
        for t in range(0, runs, 4):
            weight = jnp.concatenate([jnp.concatenate([p_ref[m], p_ref[m + 1]], 1) for m in (t, t + 2)], 0)
            value = jnp.concatenate([rows[x : x + deep] for x in (t * deep // 2, t * deep // 2 + deep)], 1)
            term = jnp.dot(weight, value, preferred_element_type=jnp.float32)
            total = term if total is None else total + term
        return total[:heads, :head] + total[heads:, head:]

    def note(b, high, total):
        where, i = lax.div(b, half), lax.rem(b, half)
        table = stat[where, me]
        for x in range(2):
            rows = slice(8 * x, 8 * x + 8)
            table = jnp.where(lane == 2 * i + x, high[rows], table)
            table = jnp.where(lane == 64 + 2 * i + x, total[rows], table)
        stat[where, me] = table

    def send(buf, g, s, recv):
        for r in range(1, n):
            pltpu.make_async_remote_copy(
                src_ref=buf.at[g, me],
                dst_ref=buf.at[g, me],
                send_sem=send_sem.at[s],
                recv_sem=recv.at[g],
                device_id={"sp": lax.rem(me + r, n)},
                device_id_type=pl.DeviceIdType.MESH,
            ).start()

    def arrived(buf, g, recv):
        pltpu.make_async_copy(buf.at[g, : n - 1], buf.at[g, : n - 1], recv.at[g]).wait()

    def shares(where):
        tables = [stat[where, d] for d in range(n)]
        high = functools.reduce(jnp.maximum, tables)
        counts = [jnp.exp2(t - high) for t in tables]
        total = functools.reduce(jnp.add, [pltpu.roll(t, 64, 1) * c for t, c in zip(tables, counts)])
        return [c / total for c in counts]

    def together(parts, share, b):
        out = []
        for x in range(2):
            column = 2 * (b % half) + x
            terms = [parts[d].astype(jnp.float32)[8 * x : 8 * x + 8] * share[d][:, column : column + 1] for d in range(n)]
            out.append(functools.reduce(jnp.add, terms))
        o_ref[b] = jnp.concatenate(out, 0).astype(jnp.bfloat16)

    fetch_q = pltpu.make_async_copy(q_hbm, q_ref, q_sem)
    k_copy(0).start()
    fetch_q.start()
    for b in range(1, LAG + PAIR):
        k_copy(b).start()
    for b in range(PAIR):
        v_copy(b).start()
    barrier = pltpu.get_barrier_semaphore()
    for r in range(1, n):
        pl.semaphore_signal(barrier, inc=1, device_id={"sp": lax.rem(me + r, n)}, device_id_type=pl.DeviceIdType.MESH)
    for where in range(2):
        stat[where, me] = jnp.zeros((8, 128), jnp.float32)
    fetch_q.wait()

    for b in range(0, LAG, PAIR):
        for u in range(PAIR):
            k_copy(b + u).wait()
        for u in range(PAIR):
            high = scores(b + u, s_buf.at[u])
            note(b + u, high, weights(high, s_buf.at[u], p_buf.at[b + u]))
        for u in range(PAIR):
            k_copy(b + SLOTS + u).start()
        for u in range(PAIR):
            v_copy(b + PAIR + u).start()
    pl.semaphore_wait(barrier, n - 1)

    def pair(it, _):
        b = it * PAIR
        for u in range(PAIR):
            k_copy(b + LAG + u).wait()
            v_copy(b + u).wait()
        for u in range(PAIR):
            p_ref = p_buf.at[lax.rem(it, LAG // PAIR) * PAIR + u]
            high = scores(b + LAG + u, s_buf.at[u])
            part[it, me, u * heads : (u + 1) * heads] = values(b + u, p_ref).astype(jnp.bfloat16)
            note(b + LAG + u, high, weights(high, s_buf.at[u], p_ref))

        @pl.when(b + LAG + SLOTS < batch)
        def _():
            for u in range(PAIR):
                k_copy(b + LAG + SLOTS + u).start()

        @pl.when(b + SLOTS < batch)
        def _():
            for u in range(PAIR):
                v_copy(b + SLOTS + u).start()

        send(part, it, 0, part_sem)

        @pl.when(b + LAG + PAIR == half)
        def _():
            send(stat, 0, 2, stat_sem)

        return 0

    loops = (batch - LAG) // PAIR
    lax.fori_loop(0, loops, pair, 0)
    send(stat, 1, 2, stat_sem)
    for it in range(loops, pairs):
        b = it * PAIR
        for u in range(PAIR):
            v_copy(b + u).wait()
        for u in range(PAIR):
            part[it, me, u * heads : (u + 1) * heads] = values(b + u, p_buf.at[(b + u) % LAG]).astype(jnp.bfloat16)
        send(part, it, 0, part_sem)
    for u in range(PAIR):
        b = pairs * PAIR + u
        v_copy(b).wait()
        last[u, me] = values(b, p_buf.at[b % LAG]).astype(jnp.bfloat16)
        send(last, u, 1, last_sem)

    for where in range(2):
        arrived(stat, where, stat_sem)
        share = shares(where)
        first, end = where * half // PAIR, min((where + 1) * half // PAIR, pairs)
        for it in range(first, end):
            arrived(part, it, part_sem)
        for it in range(first, end):
            for u in range(PAIR):
                together([part[it, d, u * heads : (u + 1) * heads] for d in range(n)], share, it * PAIR + u)
    for u in range(PAIR):
        arrived(last, u, last_sem)
        together([last[u, d] for d in range(n)], share, pairs * PAIR + u)
    for s, buf in enumerate((part, last, stat)):
        pltpu.make_async_copy(buf.at[:, : n - 1], buf.at[:, : n - 1], send_sem.at[s]).wait()


def solution(mesh):
    n = mesh.shape["sp"]

    def step(q, k, v):
        batch, tokens, heads, head = k.shape
        pairs = batch // PAIR - 1
        anywhere = pl.BlockSpec(memory_space=pl.ANY)
        return pl.pallas_call(
            functools.partial(attend, n),
            out_shape=pltpu.VMEM(q.shape, q.dtype),
            in_specs=[anywhere] * 3,
            out_specs=pl.BlockSpec(memory_space=pltpu.VMEM),
            scratch_shapes=[
                pltpu.VMEM(q.shape, q.dtype),
                pltpu.VMEM((SLOTS, tokens, heads, head), jnp.bfloat16),
                pltpu.VMEM((SLOTS, tokens, heads, head), jnp.bfloat16),
                pltpu.VMEM((PAIR, tokens // TILE, heads, TILE * heads), jnp.float32),
                pltpu.VMEM((LAG, tokens // TILE, heads, TILE * heads), jnp.bfloat16),
                pltpu.VMEM((pairs, n, PAIR * heads, head), jnp.bfloat16),
                pltpu.VMEM((PAIR, n, heads, head), jnp.bfloat16),
                pltpu.VMEM((2, n, 8, 128), jnp.float32),
                pltpu.SemaphoreType.DMA(()),
                pltpu.SemaphoreType.DMA((SLOTS,)),
                pltpu.SemaphoreType.DMA((SLOTS,)),
                pltpu.SemaphoreType.DMA((3,)),
                pltpu.SemaphoreType.DMA((pairs,)),
                pltpu.SemaphoreType.DMA((PAIR,)),
                pltpu.SemaphoreType.DMA((2,)),
            ],
            compiler_params=pltpu.CompilerParams(
                vmem_limit_bytes=56 << 20, collective_id=0, has_side_effects=True
            ),
            name="attend",
        )(q, k, v)

    return jax.shard_map(
        step,
        mesh=mesh,
        in_specs=(P("dp", None, None), P("dp", "sp", None, None), P("dp", "sp", None, None)),
        out_specs=P("dp", None, None),
        check_vma=False,
    )
```

time: 139 us -> 50.7 us (0.36)
  matrix products: 64.5 us -> 0 us
  Pallas kernels: 0 us -> 49.9 us
  waiting for transfers between devices: 49.4 us -> 0 us
  between operations: 13.4 us -> 0.01 us
  other arithmetic: 9.52 us -> 0 us
  local copies, waits for them, and re-layouts: 2.08 us -> 0.66 us
    dot_general x2 -> x0, matrix products: 64.5 us -> none  [einsum(): return jnp.einsum(form, a.astype(jnp.float32), b.astype(jnp.float32))]
    pallas_call x0 -> x1, Pallas kernels: none -> 49.9 us  [step(): pl.pallas_call(functools.partial(attend, n), out_shape=pltpu.VMEM(q.shape...]
    all_gather x1 -> x0, waiting for transfers between devices: 49.4 us -> none  [step(): return together(lax.all_gather(part_of(q, k, v), 'sp')).reshape(q.shape)]
    reduce_sum x2 -> x0, other arithmetic: 5 us -> none  [the longest x1 2.99 us: together(): jnp.sum(total * scale, 0)]
    reduce_max x2 -> x0, other arithmetic: 2.46 us -> none  [the longest x1 2.29 us: together(): scale = jnp.exp(high - jnp.max(high, 0))]
    mul x1 -> x0, local copies, waits for them, and re-layouts: 1.56 us -> none  [together(): seen * scale]
  transfers between devices with their start and end apart: 1 -> 0, of which waited for: 1 -> 0; matrix products, arithmetic and copies ran while one was open for 0% -> 0% of each run, Pallas kernels for 0% -> 0%
where the time goes in v2:
time: 50.7 us; the launch traced here: 50.6 us
  Pallas kernels  49.9 us (98%)
  local copies, waits for them, and re-layouts  0.66 us (1%)
    pallas_call x1, Pallas kernels, step(): pl.pallas_call(functools.partial(attend, n), out_shape=pltpu.VMEM(q.shape...  49.9 us

profile of v2, /device:TPU:0, one launch (start us, length us, event | category | flops | bytes accessed | tf_op | source)
XLA Modules:
  0.0 50.6 jit_solution(16018348435643929092)
XLA Ops:
  0.0 49.9 %attend.1 = bf16[32,16,128]{2,1,0:T(8,128)(2,1)S(1)} custom-call(bf16[32,16,128]{2,1,0:T(8,128)(2,1)} %q_hbm.1, bf16[32,512,16,128]{3,2,1,0:T(8,128)(2,1)} %k_hbm.1, bf16[32,512,16,128]{3,2,1,0:T(8,128)(2,1)} %v_hbm.1), custom_call_target="tpu_custom_call" | custom-call | tf_op jit(solution)/shard_map/attend/pallas_call | solution.py:209
  49.9 0.7 %copy.5 = bf16[32,16,128]{2,1,0:T(8,128)(2,1)} copy(bf16[32,16,128]{2,1,0:T(8,128)(2,1)S(1)} %attend.1) | data formatting | bytes 262144

commit v3 on v2

--- a/solution.py
+++ b/solution.py
@@ -13,6 +13,7 @@
 PAIR = 2
 LAG = 6
 SLOTS = 8
+BEHIND = 4
 
 
 def attend(n, q_hbm, k_hbm, v_hbm, o_ref, q_ref, k_buf, v_buf, s_buf, p_buf, part, last, stat, q_sem, k_sem, v_sem,
@@ -21,7 +22,10 @@
     runs = tokens // TILE
     pairs = batch // PAIR - 1
     half = batch // 2
-    me = lax.axis_index("sp")
+    chips = n // 2
+    chip, core = lax.div(lax.axis_index("sp"), 2), lax.rem(lax.axis_index("sp"), 2)
+    me = core * chips + chip
+    other = {"sp": 2 * chip + 1 - core}
     scale = head**-0.5 / math.log(2)
     lanes = lax.broadcasted_iota(jnp.int32, (heads, TILE * heads), 1)
     mine = lanes % heads == lax.broadcasted_iota(jnp.int32, (heads, TILE * heads), 0)
@@ -31,9 +35,24 @@
         slot = lax.rem(b, SLOTS)
         return pltpu.make_async_copy(k_hbm.at[b], k_buf.at[slot], k_sem.at[slot])
 
-    def v_copy(b):
-        slot = lax.rem(b, SLOTS)
-        return pltpu.make_async_copy(v_hbm.at[b], v_buf.at[slot], v_sem.at[slot])
+    def v_copies(b):
+        slot, part_of = lax.rem(b, SLOTS), tokens // 2
+        return [
+            pltpu.make_async_copy(
+                v_hbm.at[b, x * part_of : (x + 1) * part_of],
+                v_buf.at[slot, x * part_of : (x + 1) * part_of],
+                v_sem.at[slot, x],
+            )
+            for x in range(2)
+        ]
+
+    def fetch_v(b):
+        for copy in v_copies(b):
+            copy.start()
+
+    def fetched_v(b):
+        for copy in v_copies(b):
+            copy.wait()
 
     def scores(b, s_ref):
         keys = k_buf.at[lax.rem(b, SLOTS)].reshape(runs, TILE, heads, head)
@@ -63,11 +82,13 @@
             p_ref[m] = weight.astype(jnp.bfloat16)
         return jnp.sum(total, 1, keepdims=True)
 
-    def values(b, p_ref):
+    def values(b, p_ref, arrivals=()):
         rows = v_buf.at[lax.rem(b, SLOTS)].reshape(tokens * heads, head)
         deep = 2 * TILE * heads
         total = None
         for t in range(0, runs, 4):
+            if arrivals and t % (runs // len(arrivals)) == 0:
+                arrivals[t * len(arrivals) // runs].wait()
             weight = jnp.concatenate([jnp.concatenate([p_ref[m], p_ref[m + 1]], 1) for m in (t, t + 2)], 0)
             value = jnp.concatenate([rows[x : x + deep] for x in (t * deep // 2, t * deep // 2 + deep)], 1)
             term = jnp.dot(weight, value, preferred_element_type=jnp.float32)
@@ -83,19 +104,28 @@
             table = jnp.where(lane == 64 + 2 * i + x, total[rows], table)
         stat[where, me] = table
 
+    def remote(ref, to, s, recv):
+        pltpu.make_async_remote_copy(
+            src_ref=ref, dst_ref=ref, send_sem=send_sem.at[s], recv_sem=recv, device_id=to,
+            device_id_type=pl.DeviceIdType.MESH,
+        ).start()
+
     def send(buf, g, s, recv):
-        for r in range(1, n):
-            pltpu.make_async_remote_copy(
-                src_ref=buf.at[g, me],
-                dst_ref=buf.at[g, me],
-                send_sem=send_sem.at[s],
-                recv_sem=recv.at[g],
-                device_id={"sp": lax.rem(me + r, n)},
-                device_id_type=pl.DeviceIdType.MESH,
-            ).start()
+        for r in range(1, chips):
+            remote(buf.at[g, me], {"sp": 2 * lax.rem(chip + r, chips) + core}, s, recv.at[0, g])
+
+    def hand_on(buf, g, s, recv):
+        pltpu.make_async_copy(buf.at[g, : chips - 1], buf.at[g, : chips - 1], recv.at[0, g]).wait()
+        remote(buf.at[g, pl.ds(core * chips, chips)], other, s, recv.at[1, g])
 
     def arrived(buf, g, recv):
-        pltpu.make_async_copy(buf.at[g, : n - 1], buf.at[g, : n - 1], recv.at[g]).wait()
+        pltpu.make_async_copy(buf.at[g, :chips], buf.at[g, :chips], recv.at[1, g]).wait()
+
+    def send_all(u):
+        for r in range(1, chips):
+            for c in (core, 1 - core):
+                remote(last.at[u, me], {"sp": 2 * lax.rem(chip + r, chips) + c}, 2, last_sem.at[u])
+        remote(last.at[u, me], other, 2, last_sem.at[u])
 
     def shares(where):
         tables = [stat[where, d] for d in range(n)]
@@ -118,10 +148,11 @@
     for b in range(1, LAG + PAIR):
         k_copy(b).start()
     for b in range(PAIR):
-        v_copy(b).start()
+        fetch_v(b)
     barrier = pltpu.get_barrier_semaphore()
     for r in range(1, n):
-        pl.semaphore_signal(barrier, inc=1, device_id={"sp": lax.rem(me + r, n)}, device_id_type=pl.DeviceIdType.MESH)
+        peer = {"sp": lax.rem(lax.axis_index("sp") + r, n)}
+        pl.semaphore_signal(barrier, inc=1, device_id=peer, device_id_type=pl.DeviceIdType.MESH)
     for where in range(2):
         stat[where, me] = jnp.zeros((8, 128), jnp.float32)
     fetch_q.wait()
@@ -135,14 +166,14 @@
         for u in range(PAIR):
             k_copy(b + SLOTS + u).start()
         for u in range(PAIR):
-            v_copy(b + PAIR + u).start()
+            fetch_v(b + PAIR + u)
     pl.semaphore_wait(barrier, n - 1)
 
     def pair(it, _):
         b = it * PAIR
         for u in range(PAIR):
             k_copy(b + LAG + u).wait()
-            v_copy(b + u).wait()
+            fetched_v(b + u)
         for u in range(PAIR):
             p_ref = p_buf.at[lax.rem(it, LAG // PAIR) * PAIR + u]
             high = scores(b + LAG + u, s_buf.at[u])
@@ -157,32 +188,41 @@
         @pl.when(b + SLOTS < batch)
         def _():
             for u in range(PAIR):
-                v_copy(b + SLOTS + u).start()
+                fetch_v(b + SLOTS + u)
 
         send(part, it, 0, part_sem)
 
         @pl.when(b + LAG + PAIR == half)
         def _():
-            send(stat, 0, 2, stat_sem)
+            send(stat, 0, 1, stat_sem)
+
+        @pl.when(it >= BEHIND)
+        def _():
+            hand_on(part, it - BEHIND, 0, part_sem)
 
         return 0
 
     loops = (batch - LAG) // PAIR
     lax.fori_loop(0, loops, pair, 0)
-    send(stat, 1, 2, stat_sem)
+    send(stat, 1, 1, stat_sem)
     for it in range(loops, pairs):
         b = it * PAIR
         for u in range(PAIR):
-            v_copy(b + u).wait()
+            fetched_v(b + u)
         for u in range(PAIR):
             part[it, me, u * heads : (u + 1) * heads] = values(b + u, p_buf.at[(b + u) % LAG]).astype(jnp.bfloat16)
         send(part, it, 0, part_sem)
     for u in range(PAIR):
         b = pairs * PAIR + u
-        v_copy(b).wait()
-        last[u, me] = values(b, p_buf.at[b % LAG]).astype(jnp.bfloat16)
-        send(last, u, 1, last_sem)
-
+        last[u, me] = values(b, p_buf.at[b % LAG], v_copies(b)).astype(jnp.bfloat16)
+        send_all(u)
+
+    hand_on(stat, 0, 1, stat_sem)
+    for it in range(loops - BEHIND, pairs - 2):
+        hand_on(part, it, 0, part_sem)
+    hand_on(stat, 1, 1, stat_sem)
+    for it in range(pairs - 2, pairs):
+        hand_on(part, it, 0, part_sem)
     for where in range(2):
         arrived(stat, where, stat_sem)
         share = shares(where)
@@ -193,10 +233,10 @@
             for u in range(PAIR):
                 together([part[it, d, u * heads : (u + 1) * heads] for d in range(n)], share, it * PAIR + u)
     for u in range(PAIR):
-        arrived(last, u, last_sem)
+        pltpu.make_async_copy(last.at[u, : n - 1], last.at[u, : n - 1], last_sem.at[u]).wait()
         together([last[u, d] for d in range(n)], share, pairs * PAIR + u)
-    for s, buf in enumerate((part, last, stat)):
-        pltpu.make_async_copy(buf.at[:, : n - 1], buf.at[:, : n - 1], send_sem.at[s]).wait()
+    for s, buf, sent in ((0, part, n - 1), (1, stat, n - 1), (2, last, n - 1)):
+        pltpu.make_async_copy(buf.at[:, :sent], buf.at[:, :sent], send_sem.at[s]).wait()
 
 
 def solution(mesh):
@@ -222,11 +262,11 @@
                 pltpu.VMEM((2, n, 8, 128), jnp.float32),
                 pltpu.SemaphoreType.DMA(()),
                 pltpu.SemaphoreType.DMA((SLOTS,)),
-                pltpu.SemaphoreType.DMA((SLOTS,)),
+                pltpu.SemaphoreType.DMA((SLOTS, 2)),
                 pltpu.SemaphoreType.DMA((3,)),
-                pltpu.SemaphoreType.DMA((pairs,)),
+                pltpu.SemaphoreType.DMA((2, pairs)),
                 pltpu.SemaphoreType.DMA((PAIR,)),
-                pltpu.SemaphoreType.DMA((2,)),
+                pltpu.SemaphoreType.DMA((2, 2)),
             ],
             compiler_params=pltpu.CompilerParams(
                 vmem_limit_bytes=56 << 20, collective_id=0, has_side_effects=True

time: 50.7 us -> 49.3 us (0.972)
  Pallas kernels: 49.9 us -> 48.4 us
    pallas_call x1, Pallas kernels: 49.9 us -> 48.4 us  [step(): pl.pallas_call(functools.partial(attend, n), out_shape=pltpu.VMEM(q.shape...]
where the time goes in v3:
time: 49.3 us; the launch traced here: 49.1 us
  Pallas kernels  48.4 us (98%)
  local copies, waits for them, and re-layouts  0.66 us (1%)
    pallas_call x1, Pallas kernels, step(): pl.pallas_call(functools.partial(attend, n), out_shape=pltpu.VMEM(q.shape...  48.4 us

profile of v3, /device:TPU:0, one launch (start us, length us, event | category | flops | bytes accessed | tf_op | source)
XLA Modules:
  0.0 49.1 jit_solution(16452387630733905608)
XLA Ops:
  0.0 48.4 %attend.1 = bf16[32,16,128]{2,1,0:T(8,128)(2,1)S(1)} custom-call(bf16[32,16,128]{2,1,0:T(8,128)(2,1)} %q_hbm.1, bf16[32,512,16,128]{3,2,1,0:T(8,128)(2,1)} %k_hbm.1, bf16[32,512,16,128]{3,2,1,0:T(8,128)(2,1)} %v_hbm.1), custom_call_target="tpu_custom_call" | custom-call | tf_op jit(solution)/shard_map/attend/pallas_call | solution.py:249
  48.5 0.7 %copy.5 = bf16[32,16,128]{2,1,0:T(8,128)(2,1)} copy(bf16[32,16,128]{2,1,0:T(8,128)(2,1)S(1)} %attend.1) | data formatting | bytes 262144

commit v4 on v3

--- a/solution.py
+++ b/solution.py
@@ -12,7 +12,9 @@
 STEP = 32
 PAIR = 2
 LAG = 6
-SLOTS = 8
+K_SLOTS = 8
+V_SLOTS = 8
+CUT = 1
 BEHIND = 4
 
 
@@ -32,18 +34,18 @@
     lane = lax.broadcasted_iota(jnp.int32, (8, 128), 1)
 
     def k_copy(b):
-        slot = lax.rem(b, SLOTS)
+        slot = lax.rem(b, K_SLOTS)
         return pltpu.make_async_copy(k_hbm.at[b], k_buf.at[slot], k_sem.at[slot])
 
     def v_copies(b):
-        slot, part_of = lax.rem(b, SLOTS), tokens // 2
+        slot, part_of = lax.rem(b, V_SLOTS), tokens // CUT
         return [
             pltpu.make_async_copy(
                 v_hbm.at[b, x * part_of : (x + 1) * part_of],
                 v_buf.at[slot, x * part_of : (x + 1) * part_of],
                 v_sem.at[slot, x],
             )
-            for x in range(2)
+            for x in range(CUT)
         ]
 
     def fetch_v(b):
@@ -55,7 +57,7 @@
             copy.wait()
 
     def scores(b, s_ref):
-        keys = k_buf.at[lax.rem(b, SLOTS)].reshape(runs, TILE, heads, head)
+        keys = k_buf.at[lax.rem(b, K_SLOTS)].reshape(runs, TILE, heads, head)
         query = q_ref[b]
         none = jnp.zeros_like(query)
         high = jnp.full((heads, TILE * heads), -jnp.inf, jnp.float32)
@@ -83,7 +85,7 @@
         return jnp.sum(total, 1, keepdims=True)
 
     def values(b, p_ref, arrivals=()):
-        rows = v_buf.at[lax.rem(b, SLOTS)].reshape(tokens * heads, head)
+        rows = v_buf.at[lax.rem(b, V_SLOTS)].reshape(tokens * heads, head)
         deep = 2 * TILE * heads
         total = None
         for t in range(0, runs, 4):
@@ -145,9 +147,9 @@
     fetch_q = pltpu.make_async_copy(q_hbm, q_ref, q_sem)
     k_copy(0).start()
     fetch_q.start()
-    for b in range(1, LAG + PAIR):
+    for b in range(1, K_SLOTS):
         k_copy(b).start()
-    for b in range(PAIR):
+    for b in range(V_SLOTS - LAG):
         fetch_v(b)
     barrier = pltpu.get_barrier_semaphore()
     for r in range(1, n):
@@ -164,9 +166,10 @@
             high = scores(b + u, s_buf.at[u])
             note(b + u, high, weights(high, s_buf.at[u], p_buf.at[b + u]))
         for u in range(PAIR):
-            k_copy(b + SLOTS + u).start()
-        for u in range(PAIR):
-            fetch_v(b + PAIR + u)
+            k_copy(b + K_SLOTS + u).start()
+        for u in range(PAIR):
+            if b + V_SLOTS >= LAG:
+                fetch_v(b + V_SLOTS - LAG + u)
     pl.semaphore_wait(barrier, n - 1)
 
     def pair(it, _):
@@ -180,15 +183,15 @@
             part[it, me, u * heads : (u + 1) * heads] = values(b + u, p_ref).astype(jnp.bfloat16)
             note(b + LAG + u, high, weights(high, s_buf.at[u], p_ref))
 
-        @pl.when(b + LAG + SLOTS < batch)
+        @pl.when(b + LAG + K_SLOTS < batch)
         def _():
             for u in range(PAIR):
-                k_copy(b + LAG + SLOTS + u).start()
-
-        @pl.when(b + SLOTS < batch)
+                k_copy(b + LAG + K_SLOTS + u).start()
+
+        @pl.when(b + V_SLOTS < batch)
         def _():
             for u in range(PAIR):
-                fetch_v(b + SLOTS + u)
+                fetch_v(b + V_SLOTS + u)
 
         send(part, it, 0, part_sem)
 
@@ -217,21 +220,26 @@
         last[u, me] = values(b, p_buf.at[b % LAG], v_copies(b)).astype(jnp.bfloat16)
         send_all(u)
 
-    hand_on(stat, 0, 1, stat_sem)
-    for it in range(loops - BEHIND, pairs - 2):
-        hand_on(part, it, 0, part_sem)
-    hand_on(stat, 1, 1, stat_sem)
-    for it in range(pairs - 2, pairs):
-        hand_on(part, it, 0, part_sem)
-    for where in range(2):
-        arrived(stat, where, stat_sem)
-        share = shares(where)
-        first, end = where * half // PAIR, min((where + 1) * half // PAIR, pairs)
+    def combine(share, first, end):
         for it in range(first, end):
             arrived(part, it, part_sem)
         for it in range(first, end):
             for u in range(PAIR):
                 together([part[it, d, u * heads : (u + 1) * heads] for d in range(n)], share, it * PAIR + u)
+
+    middle, late = half // PAIR, pairs - 2
+    hand_on(stat, 0, 1, stat_sem)
+    arrived(stat, 0, stat_sem)
+    combine(shares(0), 0, middle)
+    for it in range(loops - BEHIND, late):
+        hand_on(part, it, 0, part_sem)
+    hand_on(stat, 1, 1, stat_sem)
+    for it in range(late, pairs):
+        hand_on(part, it, 0, part_sem)
+    arrived(stat, 1, stat_sem)
+    share = shares(1)
+    combine(share, middle, late)
+    combine(share, late, pairs)
     for u in range(PAIR):
         pltpu.make_async_copy(last.at[u, : n - 1], last.at[u, : n - 1], last_sem.at[u]).wait()
         together([last[u, d] for d in range(n)], share, pairs * PAIR + u)
@@ -253,16 +261,16 @@
             out_specs=pl.BlockSpec(memory_space=pltpu.VMEM),
             scratch_shapes=[
                 pltpu.VMEM(q.shape, q.dtype),
-                pltpu.VMEM((SLOTS, tokens, heads, head), jnp.bfloat16),
-                pltpu.VMEM((SLOTS, tokens, heads, head), jnp.bfloat16),
+                pltpu.VMEM((K_SLOTS, tokens, heads, head), jnp.bfloat16),
+                pltpu.VMEM((V_SLOTS, tokens, heads, head), jnp.bfloat16),
                 pltpu.VMEM((PAIR, tokens // TILE, heads, TILE * heads), jnp.float32),
                 pltpu.VMEM((LAG, tokens // TILE, heads, TILE * heads), jnp.bfloat16),
                 pltpu.VMEM((pairs, n, PAIR * heads, head), jnp.bfloat16),
                 pltpu.VMEM((PAIR, n, heads, head), jnp.bfloat16),
                 pltpu.VMEM((2, n, 8, 128), jnp.float32),
                 pltpu.SemaphoreType.DMA(()),
-                pltpu.SemaphoreType.DMA((SLOTS,)),
-                pltpu.SemaphoreType.DMA((SLOTS, 2)),
+                pltpu.SemaphoreType.DMA((K_SLOTS,)),
+                pltpu.SemaphoreType.DMA((V_SLOTS, CUT)),
                 pltpu.SemaphoreType.DMA((3,)),
                 pltpu.SemaphoreType.DMA((2, pairs)),
                 pltpu.SemaphoreType.DMA((PAIR,)),

time: 49.3 us -> 49.2 us (level)
  no operation moved by 1% of the time
where the time goes in v4:
time: 49.2 us; the launch traced here: 49 us
  Pallas kernels  48.4 us (98%)
  local copies, waits for them, and re-layouts  0.66 us (1%)
    pallas_call x1, Pallas kernels, step(): pl.pallas_call(functools.partial(attend, n), out_shape=pltpu.VMEM(q.shape...  48.4 us

profile of v4, /device:TPU:0, one launch (start us, length us, event | category | flops | bytes accessed | tf_op | source)
XLA Modules:
  0.0 49.0 jit_solution(4228068606495996780)
XLA Ops:
  0.0 48.4 %attend.1 = bf16[32,16,128]{2,1,0:T(8,128)(2,1)S(1)} custom-call(bf16[32,16,128]{2,1,0:T(8,128)(2,1)} %q_hbm.1, bf16[32,512,16,128]{3,2,1,0:T(8,128)(2,1)} %k_hbm.1, bf16[32,512,16,128]{3,2,1,0:T(8,128)(2,1)} %v_hbm.1), custom_call_target="tpu_custom_call" | custom-call | tf_op jit(solution)/shard_map/attend/pallas_call | solution.py:257
  48.4 0.7 %copy.5 = bf16[32,16,128]{2,1,0:T(8,128)(2,1)} copy(bf16[32,16,128]{2,1,0:T(8,128)(2,1)S(1)} %attend.1) | data formatting | bytes 262144
